TPU v7x, 32 devices: a whole 2x2x4 slice. The times are simulated.
32 devices in a mesh: dp: 8 (over z, y), tensor: 4 (over x, core).
Axes of the slice: x: 2, y: 2, z: 4, core: 2. Of those that a mesh axis runs over, the one named last changes fastest.
Arguments:
- tokens: bfloat16 [8192, 1024], P('dp'), may hold values from -6 to 6
- cotangent: bfloat16 [8192, 1024], P('dp'), may hold values from -6 to 6
- norm_params: float32 [4, 1024], replicated, may hold values from 0.25 to 1.75
- attention_weight: bfloat16 [1024, 3, 1024], P('dp', None, 'tensor'), may hold values from -0.1875 to 0.1875
- attention_bias: float32 [3, 1024], P(None, 'tensor'), may hold values from -3 to 3
- merge_weight: bfloat16 [1024, 1024], P('dp', 'tensor'), may hold values from -1.5 to 1.5
- branch_bias: float32 [2, 1024], replicated, may hold values from -3 to 3
- up_weight: bfloat16 [1024, 4096], P('dp', 'tensor'), may hold values from -0.1875 to 0.1875
- up_bias: float32 [4096], P('tensor'), may hold values from -3 to 3
- down_weight: bfloat16 [1024, 4096], P('dp', 'tensor'), may hold values from -0.09375 to 0.09375
- prefix_ids: int32 [10], replicated, may hold values from 0 to 9, each once
- prefix_table: float32 [10, 1024], replicated, may hold values from -1.25 to 1.25
- encoder_weight: float32 [1024, 512], P('dp'), may hold values from -0.625 to 0.625
- encoder_bias: float32 [512], replicated, may hold values from -0.625 to 0.625
- decoder_weight: float32 [512, 2, 1024], P('dp', None, 'tensor'), may hold values from -0.625 to 0.625
- decoder_bias: float32 [2, 1024], P(None, 'tensor'), may hold values from -0.625 to 0.625
- first_table: float32 [10, 1024], replicated, may hold values from -1.9073486e-06 to 1.9073486e-06
- second_table: float32 [10, 1024], replicated, may hold values from 5.3138434e-15 to 8.5369944e-14
- first_encoder: float32 [1024, 512], P('dp'), may hold values from -5.9604645e-07 to 5.9604645e-07
- second_encoder: float32 [1024, 512], P('dp'), may hold values from 3.8329363e-16 to 6.0978533e-15
- first_encoder_bias: float32 [512], replicated, may hold values from -3.33786e-06 to 3.33786e-06
- second_encoder_bias: float32 [512], replicated, may hold values from 1.0540575e-14 to 1.6899766e-13
- first_decoder: float32 [512, 2, 1024], P('dp', None, 'tensor'), may hold values from -4.7683716e-07 to 4.7683716e-07
- second_decoder: float32 [512, 2, 1024], P('dp', None, 'tensor'), may hold values from 2.230072e-16 to 3.5716e-15
- first_decoder_bias: float32 [2, 1024], P(None, 'tensor'), may hold values from -9.536743e-07 to 9.536743e-07
- second_decoder_bias: float32 [2, 1024], P(None, 'tensor'), may hold values from 8.885443e-16 to 1.42864e-14
Outputs:
- output: bfloat16 [8192, 1024], P(('dp', 'tensor'))
- input_grad: bfloat16 [8192, 1024], P(('dp', 'tensor'))
- grad_norm: float32 [], replicated
- new_table: float32 [10, 1024], replicated
- new_first_table: float32 [10, 1024], replicated
- new_second_table: float32 [10, 1024], replicated
- new_encoder: float32 [1024, 512], P('dp')
- new_first_encoder: float32 [1024, 512], P('dp')
- new_second_encoder: float32 [1024, 512], P('dp')
- new_encoder_bias: float32 [512], replicated
- new_first_encoder_bias: float32 [512], replicated
- new_second_encoder_bias: float32 [512], replicated
- new_decoder: float32 [512, 2, 1024], P('dp', None, 'tensor')
- new_first_decoder: float32 [512, 2, 1024], P('dp', None, 'tensor')
- new_second_decoder: float32 [512, 2, 1024], P('dp', None, 'tensor')
- new_decoder_bias: float32 [2, 1024], P(None, 'tensor')
- new_first_decoder_bias: float32 [2, 1024], P(None, 'tensor')
- new_second_decoder_bias: float32 [2, 1024], P(None, 'tensor')
Inputs may be any that keep to these rules, and one draw needn't show every extreme that they name: `prefix_ids`: every table row is used by exactly one prefix position.
All inputs are finite; a program needn't handle non-finite values.
Results may differ from a plain program's by a relative error of at most 0.017.
Values may be sent and summed in bfloat16 or wider, within the bound.
No kernel may reach another device: no remote copies, remote signals or barrier semaphores. Data moves between devices by JAX's collectives and lax.ppermute only.
A program may use at most 128 MiB of HBM per device.

v0:
```python
import jax
import jax.numpy as jnp
from jax import lax
from jax.sharding import PartitionSpec as P

HD = 64
PRE = 10
SEQ = 1024
STEP = 10
NORM_EPS = 1e-05
CLIP_LIMIT = 0.001
LEARN_RATE = 0.05
WEIGHT_DECAY = 0.01
BETA_FIRST = 0.9
BETA_SECOND = 0.999
ADAM_EPS = 1e-08
MASKED = -1e30
GELU_COEF = 0.7978845608028654


def layer_norm(rows, gain, shift):
    center = jnp.mean(rows, axis=-1, keepdims=True)
    offsets = rows - center
    spread = jnp.mean(offsets * offsets, axis=-1, keepdims=True)
    return offsets * lax.rsqrt(spread + NORM_EPS) * gain + shift


def norm_back(rows, gain, shift, grad_rows):
    _, pull_back = jax.vjp(lambda values: layer_norm(values, gain, shift), rows)
    return pull_back(grad_rows)[0]


def gelu_tanh(values):
    return (
        0.5 * values * (1.0 + jnp.tanh(GELU_COEF * (values + 0.044715 * values * values * values)))
    )


def adam_update(weight, grad, first, second, factor):
    clipped = grad * factor
    new_first = BETA_FIRST * first + (1.0 - BETA_FIRST) * clipped
    new_second = BETA_SECOND * second + (1.0 - BETA_SECOND) * clipped * clipped
    fix_first = 1.0 - BETA_FIRST**STEP
    fix_second = 1.0 - BETA_SECOND**STEP
    new_weight = weight * (1.0 - LEARN_RATE * WEIGHT_DECAY) - LEARN_RATE * (
        new_first / fix_first
    ) / (jnp.sqrt(new_second / fix_second) + ADAM_EPS)
    return (new_weight, new_first, new_second)


def score_blocks(query_rows, keys, prefix_keys, offset, finish, score_scale):
    pre_scores = (
        jnp.einsum("qhe,jhe->hqj", query_rows, prefix_keys, preferred_element_type=jnp.float32)
        * score_scale
    )
    own_scores = (
        jnp.einsum("qhe,khe->hqk", query_rows, keys[:finish], preferred_element_type=jnp.float32)
        * score_scale
    )
    visible = (offset + jnp.arange(finish - offset))[:, None] >= jnp.arange(finish)[None, :]
    own_scores = jnp.where(visible[None], own_scores, MASKED)
    return (pre_scores, own_scores)


def attend_forward(queries, keys, values, prefix_keys, prefix_values):
    length = queries.shape[0]
    block_rows = min(512, length)
    score_scale = float(queries.shape[2]) ** (-0.5)
    mixtures = []
    log_sums = []
    for offset in range(0, length, block_rows):
        finish = offset + block_rows
        pre_scores, own_scores = score_blocks(
            queries[offset:finish], keys, prefix_keys, offset, finish, score_scale
        )
        highest = jnp.maximum(jnp.max(pre_scores, -1), jnp.max(own_scores, -1))
        pre_exp = jnp.exp(pre_scores - highest[..., None])
        own_exp = jnp.exp(own_scores - highest[..., None])
        totals = jnp.sum(pre_exp, -1) + jnp.sum(own_exp, -1)
        pre_prob = (pre_exp / totals[..., None]).astype(jnp.bfloat16)
        own_prob = (own_exp / totals[..., None]).astype(jnp.bfloat16)
        mixture = jnp.einsum(
            "hqj,jhe->qhe", pre_prob, prefix_values, preferred_element_type=jnp.float32
        )
        mixture = mixture + jnp.einsum(
            "hqk,khe->qhe", own_prob, values[:finish], preferred_element_type=jnp.float32
        )
        mixtures.append(mixture)
        log_sums.append(highest + jnp.log(totals))
    return (jnp.concatenate(mixtures, 0), jnp.concatenate(log_sums, 1))


def attend_backward(queries, keys, values, prefix_keys, prefix_values, grad_out, log_sums):
    length = queries.shape[0]
    block_rows = min(512, length)
    score_scale = float(queries.shape[2]) ** (-0.5)
    grad_queries = []
    grad_keys = jnp.zeros(keys.shape, jnp.float32)
    grad_values = jnp.zeros(values.shape, jnp.float32)
    grad_pre_keys = jnp.zeros(prefix_keys.shape, jnp.float32)
    grad_pre_values = jnp.zeros(prefix_values.shape, jnp.float32)
    for offset in range(0, length, block_rows):
        finish = offset + block_rows
        query_rows = queries[offset:finish]
        grad_rows = grad_out[offset:finish]
        pre_scores, own_scores = score_blocks(
            query_rows, keys, prefix_keys, offset, finish, score_scale
        )
        block_sums = log_sums[:, offset:finish, None]
        pre_prob = jnp.exp(pre_scores - block_sums)
        own_prob = jnp.exp(own_scores - block_sums)
        pre_dprob = jnp.einsum(
            "qhe,jhe->hqj", grad_rows, prefix_values, preferred_element_type=jnp.float32
        )
        own_dprob = jnp.einsum(
            "qhe,khe->hqk", grad_rows, values[:finish], preferred_element_type=jnp.float32
        )
        inner = jnp.sum(pre_prob * pre_dprob, -1) + jnp.sum(own_prob * own_dprob, -1)
        pre_dscore = (pre_prob * (pre_dprob - inner[..., None])).astype(jnp.bfloat16)
        own_dscore = (own_prob * (own_dprob - inner[..., None])).astype(jnp.bfloat16)
        grad_query = jnp.einsum(
            "hqj,jhe->qhe", pre_dscore, prefix_keys, preferred_element_type=jnp.float32
        )
        grad_query = grad_query + jnp.einsum(
            "hqk,khe->qhe", own_dscore, keys[:finish], preferred_element_type=jnp.float32
        )
        grad_queries.append(grad_query * score_scale)
        grad_keys = grad_keys.at[:finish].add(
            jnp.einsum("hqk,qhe->khe", own_dscore, query_rows, preferred_element_type=jnp.float32)
            * score_scale
        )
        grad_values = grad_values.at[:finish].add(
            jnp.einsum(
                "hqk,qhe->khe",
                own_prob.astype(jnp.bfloat16),
                grad_rows,
                preferred_element_type=jnp.float32,
            )
        )
        grad_pre_keys = (
            grad_pre_keys
            + jnp.einsum("hqj,qhe->jhe", pre_dscore, query_rows, preferred_element_type=jnp.float32)
            * score_scale
        )
        grad_pre_values = grad_pre_values + jnp.einsum(
            "hqj,qhe->jhe",
            pre_prob.astype(jnp.bfloat16),
            grad_rows,
            preferred_element_type=jnp.float32,
        )
    grad_seq = jnp.stack([jnp.concatenate(grad_queries, 0), grad_keys, grad_values], 1)
    grad_prefix = jnp.stack([grad_pre_keys, grad_pre_values], 1)
    return (grad_seq, grad_prefix)


def on_device(
    tokens,
    cotangent,
    norm_params,
    attention_weight,
    attention_bias,
    merge_weight,
    branch_bias,
    up_weight,
    up_bias,
    down_weight,
    prefix_ids,
    prefix_table,
    encoder_weight,
    encoder_bias,
    decoder_weight,
    decoder_bias,
    first_table,
    second_table,
    first_encoder,
    second_encoder,
    first_encoder_bias,
    second_encoder_bias,
    first_decoder,
    second_decoder,
    first_decoder_bias,
    second_decoder_bias,
):
    highest_prec = lax.Precision.HIGHEST
    dp_index = lax.axis_index("dp")
    tok_rows = tokens.shape[0]
    local_width = merge_weight.shape[1]
    local_heads = local_width // HD
    sequences = tok_rows // SEQ
    share = tok_rows // lax.axis_size("tensor")
    row_start = lax.axis_index("tensor") * share
    gathered = (
        lax.all_gather(attention_weight, "dp", axis=0, tiled=True),
        lax.all_gather(merge_weight, "dp", axis=0, tiled=True),
        lax.all_gather(up_weight, "dp", axis=0, tiled=True),
        lax.all_gather(down_weight, "dp", axis=0, tiled=True),
        lax.all_gather(encoder_weight.astype(jnp.bfloat16), "dp", axis=0, tiled=True),
        lax.all_gather(decoder_weight.astype(jnp.bfloat16), "dp", axis=0, tiled=True),
    )
    attend_full, merge_full, up_full, down_full, encoder_full, decoder_full = gathered
    onehot = (prefix_ids[:, None] == jnp.arange(PRE, dtype=jnp.int32)[None, :]).astype(jnp.float32)
    selected = jnp.dot(onehot, prefix_table, precision=highest_prec)
    selected_low = selected.astype(jnp.bfloat16)
    encoded = jnp.dot(selected_low, encoder_full, preferred_element_type=jnp.float32) + encoder_bias
    hidden_prefix = jnp.tanh(encoded)
    hidden_low = hidden_prefix.astype(jnp.bfloat16)
    prefix_kv = (
        jnp.einsum("jp,pcm->jcm", hidden_low, decoder_full, preferred_element_type=jnp.float32)
        + decoder_bias[None]
    )
    prefix_kv = prefix_kv.astype(jnp.bfloat16).reshape(PRE, 2, local_heads, HD)
    prefix_keys = prefix_kv[:, 0]
    prefix_values = prefix_kv[:, 1]
    inputs = tokens.astype(jnp.float32)

    def forward_sequence(seq_rows):
        return attend_forward(
            seq_rows[:, 0], seq_rows[:, 1], seq_rows[:, 2], prefix_keys, prefix_values
        )

    def front(attend_mat, merge_mat, up_mat):
        normed_one = layer_norm(inputs, norm_params[0], norm_params[1]).astype(jnp.bfloat16)
        projected = (
            jnp.einsum("td,dcm->tcm", normed_one, attend_mat, preferred_element_type=jnp.float32)
            + attention_bias[None]
        )
        projected = projected.astype(jnp.bfloat16).reshape(sequences, SEQ, 3, local_heads, HD)
        mixtures, log_sums = lax.map(forward_sequence, projected)
        mixture = mixtures.reshape(tok_rows, local_width).astype(jnp.bfloat16)
        merged_part = jnp.einsum(
            "tm,dm->td", mixture, merge_mat, preferred_element_type=jnp.float32
        )
        merged = lax.psum(merged_part.astype(jnp.bfloat16), "tensor").astype(jnp.float32)
        resid = inputs + merged + branch_bias[0]
        normed_two = layer_norm(resid, norm_params[2], norm_params[3]).astype(jnp.bfloat16)
        hidden_pre = jnp.dot(normed_two, up_mat, preferred_element_type=jnp.float32) + up_bias
        return (projected, log_sums, resid, hidden_pre)

    projected, log_sums, resid, hidden_pre = front(attend_full, merge_full, up_full)
    hidden_act = gelu_tanh(hidden_pre).astype(jnp.bfloat16)
    branch_part = jnp.einsum("tf,df->td", hidden_act, down_full, preferred_element_type=jnp.float32)
    branch_out = lax.psum(branch_part.astype(jnp.bfloat16), "tensor").astype(jnp.float32)
    output_rows = (
        lax.dynamic_slice_in_dim(resid, row_start, share, 0)
        + lax.dynamic_slice_in_dim(branch_out, row_start, share, 0)
        + branch_bias[1]
    )
    regathered = (
        lax.all_gather(attention_weight, "dp", axis=0, tiled=True),
        lax.all_gather(merge_weight, "dp", axis=0, tiled=True),
        lax.all_gather(up_weight, "dp", axis=0, tiled=True),
        lax.all_gather(down_weight, "dp", axis=0, tiled=True),
        lax.all_gather(encoder_weight.astype(jnp.bfloat16), "dp", axis=0, tiled=True),
        lax.all_gather(decoder_weight.astype(jnp.bfloat16), "dp", axis=0, tiled=True),
    )
    attend_back, merge_back, up_back, down_back, encoder_back, decoder_back = regathered
    projected, log_sums, resid, hidden_pre = front(attend_back, merge_back, up_back)
    grad_hidden = jnp.dot(cotangent, down_back, preferred_element_type=jnp.float32)
    _, gelu_pull = jax.vjp(gelu_tanh, hidden_pre)
    grad_pre = gelu_pull(grad_hidden)[0].astype(jnp.bfloat16)
    up_part = jnp.einsum("tf,df->td", grad_pre, up_back, preferred_element_type=jnp.float32)
    grad_output = cotangent.astype(jnp.float32)
    up_total = lax.psum(up_part.astype(jnp.bfloat16), "tensor").astype(jnp.float32)
    grad_resid = grad_output + norm_back(resid, norm_params[2], norm_params[3], up_total)
    branch_grad = grad_resid.astype(jnp.bfloat16)
    grad_mixture = jnp.dot(branch_grad, merge_back, preferred_element_type=jnp.float32).astype(
        jnp.bfloat16
    )
    grad_mixture = grad_mixture.reshape(sequences, SEQ, local_heads, HD)

    def backward_sequence(items):
        seq_rows, grad_rows, seq_sums = items
        return attend_backward(
            seq_rows[:, 0],
            seq_rows[:, 1],
            seq_rows[:, 2],
            prefix_keys,
            prefix_values,
            grad_rows,
            seq_sums,
        )

    grad_seqs, grad_prefixes = lax.map(backward_sequence, (projected, grad_mixture, log_sums))
    grad_projected = grad_seqs.reshape(tok_rows, 3, local_width).astype(jnp.bfloat16)
    first_part = jnp.einsum(
        "tcm,dcm->td", grad_projected, attend_back, preferred_element_type=jnp.float32
    )
    first_total = lax.psum(first_part.astype(jnp.bfloat16), "tensor").astype(jnp.float32)
    input_full = grad_resid + norm_back(inputs, norm_params[0], norm_params[1], first_total)
    input_grad = lax.dynamic_slice_in_dim(input_full, row_start, share, 0)
    prefix_grad = jnp.sum(grad_prefixes, 0).reshape(PRE, 2, local_width)
    prefix_total = lax.psum(prefix_grad, "dp")
    prefix_low = prefix_total.astype(jnp.bfloat16)
    grad_decoder = jnp.einsum(
        "jp,jcm->pcm", hidden_low, prefix_low, preferred_element_type=jnp.float32
    )
    grad_decoder_bias = jnp.sum(prefix_low.astype(jnp.float32), 0)
    encoded_part = jnp.einsum(
        "jcm,pcm->jp", prefix_low, decoder_back, preferred_element_type=jnp.float32
    )
    square_part = jnp.sum(grad_decoder * grad_decoder) + jnp.sum(
        grad_decoder_bias * grad_decoder_bias
    )
    encoded_grad, square_decoder = lax.psum((encoded_part, square_part), "tensor")
    grad_encoded = (encoded_grad * (1.0 - hidden_prefix * hidden_prefix)).astype(jnp.bfloat16)
    grad_encoder = jnp.dot(selected_low.T, grad_encoded, preferred_element_type=jnp.float32)
    grad_encoder_bias = jnp.sum(grad_encoded.astype(jnp.float32), 0)
    grad_selected = jnp.dot(grad_encoded, encoder_back.T, preferred_element_type=jnp.float32)
    grad_table = jnp.dot(onehot.T, grad_selected, precision=highest_prec)
    squares = (
        square_decoder
        + jnp.sum(grad_table * grad_table)
        + jnp.sum(grad_encoder * grad_encoder)
        + jnp.sum(grad_encoder_bias * grad_encoder_bias)
    )
    grad_norm = jnp.sqrt(squares)
    factor = CLIP_LIMIT / (grad_norm + 1e-06)
    encoder_rows = encoder_weight.shape[0]
    decoder_rows = decoder_weight.shape[0]
    encoder_own = lax.dynamic_slice_in_dim(grad_encoder, dp_index * encoder_rows, encoder_rows, 0)
    decoder_own = lax.dynamic_slice_in_dim(grad_decoder, dp_index * decoder_rows, decoder_rows, 0)
    table_new = adam_update(prefix_table, grad_table, first_table, second_table, factor)
    encoder_new = adam_update(encoder_weight, encoder_own, first_encoder, second_encoder, factor)
    enc_bias_new = adam_update(
        encoder_bias, grad_encoder_bias, first_encoder_bias, second_encoder_bias, factor
    )
    decoder_new = adam_update(decoder_weight, decoder_own, first_decoder, second_decoder, factor)
    dec_bias_new = adam_update(
        decoder_bias, grad_decoder_bias, first_decoder_bias, second_decoder_bias, factor
    )
    return (
        output_rows.astype(jnp.bfloat16),
        input_grad.astype(jnp.bfloat16),
        grad_norm,
        table_new[0],
        table_new[1],
        table_new[2],
        encoder_new[0],
        encoder_new[1],
        encoder_new[2],
        enc_bias_new[0],
        enc_bias_new[1],
        enc_bias_new[2],
        decoder_new[0],
        decoder_new[1],
        decoder_new[2],
        dec_bias_new[0],
        dec_bias_new[1],
        dec_bias_new[2],
    )


def solution(mesh):
    in_specs = (
        P("dp", None),
        P("dp", None),
        P(),
        P("dp", None, "tensor"),
        P(None, "tensor"),
        P("dp", "tensor"),
        P(),
        P("dp", "tensor"),
        P("tensor"),
        P("dp", "tensor"),
        P(),
        P(),
        P("dp", None),
        P(),
        P("dp", None, "tensor"),
        P(None, "tensor"),
        P(),
        P(),
        P("dp", None),
        P("dp", None),
        P(),
        P(),
        P("dp", None, "tensor"),
        P("dp", None, "tensor"),
        P(None, "tensor"),
        P(None, "tensor"),
    )
    out_specs = (
        P(("dp", "tensor"), None),
        P(("dp", "tensor"), None),
        P(),
        P(),
        P(),
        P(),
        P("dp", None),
        P("dp", None),
        P("dp", None),
        P(),
        P(),
        P(),
        P("dp", None, "tensor"),
        P("dp", None, "tensor"),
        P("dp", None, "tensor"),
        P(None, "tensor"),
        P(None, "tensor"),
        P(None, "tensor"),
    )
    return jax.shard_map(
        on_device, mesh=mesh, in_specs=in_specs, out_specs=out_specs, check_vma=False
    )
```

profile of v0, /device:TPU:0, one launch (start us, length us, event | category | flops | bytes accessed | tf_op | source)
XLA Modules:
  0.0 530.9 jit_solution(5144852693320282007)
XLA Ops:
  7.3 1.8 convert_element_type.156
  9.1 1.7 copy.65
  12.7 1.9 convert_reduce_fusion
  15.7 34.4 %all_gather.25 = bf16[512,2,256]{2,0,1:T(8,128)(2,1)S(1)} all-gather(bf16[64,2,256]{2,0,1:T(8,128)(2,1)S(1)} %copy.110), channel_id=1, replica_groups=mesh['dp'=8,'tensor'=4] {'dp'}, dimensions={0}, use_global_device_ids=true | all-gather | bytes 589824 | tf_op jit(solution)/shard_map/all_gather | solution.py:198
  50.1 31.8 %all_gather.27 = bf16[1024,256]{1,0:T(8,128)(2,1)S(1)} all-gather(bf16[128,256]{1,0:T(8,128)(2,1)S(1)} %copy-done.46), channel_id=1, replica_groups=mesh['dp'=8,'tensor'=4] {'dp'}, dimensions={0}, use_global_device_ids=true | all-gather | bytes 589824 | tf_op jit(solution)/shard_map/all_gather | solution.py:194
  83.1 1.5 fusion.86
  85.5 17.9 %all-gather.7.cloned.1.call-done = bf16[1024,3,256]{0,2,1:T(8,128)(2,1)} async-done(((bf16[128,3,256]{0,2,1:T(8,128)(2,1)}), bf16[1024,3,256]{0,2,1:T(8,128)(2,1)}) %all-gather.7.cloned.1.call-update) | async-done | bytes 1572880 | tf_op jit(solution)/shard_map/all_gather | solution.py:193
  103.4 3.4 add_convert_fusion.1
  111.0 1.8 fusion.153
  112.8 1.9 fusion
  116.1 2.5 fusion.21
  119.2 2.1 convolution_convert_fusion
  122.5 11.8 %all-reduce.10.cloned.1.call-start = ((), (), s32[]{:S(2)}) async-start(), calls=%async_computation.5 | async-start | bytes 4194304 | tf_op jit(solution)/shard_map/psum | solution.py:263
  134.9 36.1 %all-reduce.8.cloned.1.call-done = bf16[1024,1024]{1,0:T(8,128)(2,1)} async-done(((bf16[1024,1024]{1,0:T(8,128)(2,1)}), bf16[1024,1024]{1,0:T(8,128)(2,1)}) %all-reduce.8.cloned.1.call-update) | async-done | bytes 2097168 | tf_op jit(solution)/shard_map/psum | solution.py:233
  171.0 2.3 fusion.146
  173.4 1.9 copy-done.1
  175.8 46.3 %all-gather.9.cloned.1.call-done = bf16[1024,1024]{1,0:T(8,128)(2,1)} async-done(((bf16[128,1024]{1,0:T(8,128)(2,1)}), bf16[1024,1024]{1,0:T(8,128)(2,1)}) %all-gather.9.cloned.1.call-update) | async-done | bytes 2097168 | tf_op jit(solution)/shard_map/all_gather | solution.py:195
  222.2 7.2 %fusion.26 = f32[1024,1024]{1,0:T(8,128)} fusion(bf16[1024,1024]{1,0:T(8,128)(2,1)} %all-gather.9.cloned.1.call-done, f32[1024,1024]{1,0:T(8,128)} %copy-done.1, f32[1024]{0:T(1024)S(1)} %bitcast.198, f32[1024]{0:T(1024)S(1)} %bitcast.189, f32[1024]{0:T(1024)S(1)} %fusion.124, f32[1024]{0:T(1024)S(1)} %broadcast_multiply_fusion), kind=kOutput, calls=%fused_computation.54 | convolution fusion | flops 2152726528 | bytes 10502144 | tf_op jit(solution)/shard_map/dot_general | solution.py:236
  229.4 42.4 %all-gather.11.cloned.1.call-done = bf16[1024,1024]{1,0:T(8,128)(2,1)} async-done(((bf16[128,1024]{1,0:T(8,128)(2,1)}), bf16[1024,1024]{1,0:T(8,128)(2,1)}) %all-gather.11.cloned.1.call-update) | async-done | bytes 2097168 | tf_op jit(solution)/shard_map/all_gather | solution.py:196
  271.8 10.8 %fusion.45 = bf16[1024,1024]{1,0:T(8,128)(2,1)} fusion(bf16[1024,1024]{1,0:T(8,128)(2,1)} %all-gather.9.cloned.1.call-done, f32[1024,1024]{1,0:T(8,128)} %fusion.26, f32[1024]{0:T(1024)S(1)} %copy-done.62, bf16[1024,1024]{1,0:T(8,128)(2,1)} %param.39, bf16[1024,1024]{1,0:T(8,128)(2,1)} %all-gather.11.cloned.1.call-done), kind=kOutput, calls=%fused_computation.73 | convolution fusion | flops 4322230272 | bytes 12587008 | tf_op jit(solution)/shard_map/tf,df->td/dot_general | solution.py:261
  282.7 7.0 %fusion.48 = bf16[1024,1024]{1,0:T(8,128)(2,1)} fusion(bf16[1024,1024]{1,0:T(8,128)(2,1)} %all-gather.11.cloned.1.call-done, f32[1024,1024]{1,0:T(8,128)} %fusion.26, f32[1024]{0:T(1024)S(1)} %copy-done.62), kind=kOutput, calls=%fused_computation.74 | convolution fusion | flops 2159017984 | bytes 8392704 | tf_op jit(solution)/shard_map/tf,df->td/dot_general | solution.py:241
  289.7 43.0 %all-reduce.10.cloned.1.call-done = bf16[1024,1024]{1,0:T(8,128)(2,1)} async-done(((bf16[1024,1024]{1,0:T(8,128)(2,1)}), bf16[1024,1024]{1,0:T(8,128)(2,1)}) %all-reduce.10.cloned.1.call-update) | async-done | bytes 2097168 | tf_op jit(solution)/shard_map/psum | solution.py:263
  332.7 3.8 multiply_reduce_fusion.2
  337.4 1.8 fusion.138
  339.2 1.7 add_add_fusion.2
  342.4 2.4 copy-done.4
  344.7 1.6 fusion.71
  348.5 1.5 fusion.76
  352.2 4.9 multiply_reduce_fusion
  361.9 37.1 %psum.56 = bf16[10,2,256]{2,0,1:T(8,128)(2,1)S(1)} all-reduce(f32[10,2,256]{2,0,1:T(8,128)S(1)} %pad_maximum_fusion.2), channel_id=1, replica_groups=mesh['dp'=8,'tensor'=4] {'dp'}, use_global_device_ids=true, to_apply=%region_24.25 | all-reduce | flops 5120 | bytes 30720 | tf_op jit(solution)/shard_map/psum | solution.py:292
  401.0 1.9 multiply_reduce_fusion.5
  402.9 5.0 fusion.64
  409.9 6.8 %multiply_convert_fusion = bf16[4,512,1024]{2,1,0:T(8,128)(2,1)S(1)} fusion(f32[4,512,1024]{2,1,0:T(8,128)} %get-tuple-element.245, f32[4,512,1024]{2,1,0:T(8,128)} %copy-done, f32[4,512]{1,0:T(4,128)S(1)} %add.428, f32[4,512]{1,0:T(4,128)S(1)} %copy-done.27), kind=kLoop, calls=%fused_computation | loop fusion | flops 8388608 | bytes 20987904 | tf_op jit(solution)/shard_map/while/body/eval_jaxpr/convert_element_type | solution.py:120
  416.7 1.9 copy-done.6
  418.6 1.9 fusion.67
  422.1 3.8 fusion.84
  427.4 4.9 bitcast_convert_fusion
  432.4 14.0 %all-reduce.2 = (f32[]{:T(128)}, f32[10,512]{1,0:T(8,128)}) all-reduce(f32[]{:T(128)S(6)} %add.438, f32[10,512]{1,0:T(8,128)} %convolution_bitcast_fusion), channel_id=1, replica_groups=mesh['dp'=8,'tensor'=4] {'tensor'}, use_global_device_ids=true, to_apply=%region_28.29 | all-reduce | flops 5121 | bytes 40968 | tf_op jit(solution)/shard_map/psum | solution.py:304
  446.4 1.4 convert_reduce_fusion.1
  448.1 1.6 multiply_reduce_fusion.8
  451.1 2.4 multiply_reduce_fusion.4
  459.7 1.3 divide_subtract_fusion.3
  462.3 1.6 divide_subtract_fusion.2
  463.9 2.0 divide_subtract_fusion
  465.9 49.0 %all-reduce.12.cloned.1.call-done = (bf16[1024,1024]{1,0:T(8,128)(2,1)}, bf16[1024,1024]{1,0:T(8,128)(2,1)}) async-done(((bf16[1024,1024]{1,0:T(8,128)(2,1)}, bf16[1024,1024]{1,0:T(8,128)(2,1)}), (bf16[1024,1024]{1,0:T(8,128)(2,1)}, bf16[1024,1024]{1,0:T(8,128)(2,1)})) %all-reduce.12.cloned.1.call-update) | async-done | bytes 4194320 | tf_op jit(solution)/shard_map/psum | solution.py:242
  514.8 2.7 fusion.14
  517.6 1.9 fusion.145
  519.6 2.9 fusion.90
  (213 shorter events, 37.0 us)
Async XLA Ops:
  7.2 7.4 %copy-start.5 = (bf16[1024,1024]{1,0:T(8,128)(2,1)S(1)}, bf16[1024,1024]{1,0:T(8,128)(2,1)}, u32[]{:S(2)}) copy-start(bf16[1024,1024]{1,0:T(8,128)(2,1)} %param.38) | copy-start | bytes 6291460
  7.2 8.2 %copy-start.56 = (f32[4,1024]{1,0:T(4,128)S(1)}, f32[4,1024]{1,0:T(4,128)}, u32[]{:S(2)}) copy-start(f32[4,1024]{1,0:T(4,128)} %param.40) | copy-start | bytes 49156
  7.2 8.2 %copy-start.35 = (f32[10,1024]{1,0:T(8,128)S(1)}, f32[10,1024]{1,0:T(8,128)}, u32[]{:S(2)}) copy-start(f32[10,1024]{1,0:T(8,128)} %param.49) | copy-start | bytes 122884
  7.2 8.2 %copy-start.60 = (s32[10]{0:T(128)S(1)}, s32[10]{0:T(128)}, u32[]{:S(2)}) copy-start(s32[10]{0:T(128)} %param.48) | copy-start | bytes 124
  7.2 42.8 %copy-start.46 = (bf16[128,256]{1,0:T(8,128)(2,1)S(1)}, bf16[128,256]{1,0:T(8,128)(2,1)}, u32[]{:S(2)}) copy-start(bf16[128,256]{1,0:T(8,128)(2,1)} %param.43) | copy-start | bytes 196612
  7.2 75.8 %copy-start.58 = (f32[512]{0:T(512)S(1)}, f32[512]{0:T(512)}, u32[]{:S(2)}) copy-start(f32[512]{0:T(512)} %param.51) | copy-start | bytes 6148
  7.3 75.8 %all-gather.5.cloned.1.call-start = ((), (), s32[]{:S(2)}) async-start(), calls=%async_computation | async-start | bytes 1179648 | tf_op jit(solution)/shard_map/all_gather | solution.py:197
  9.1 76.1 %copy-start.57 = (f32[2,256]{1,0:T(2,128)S(1)}, f32[2,256]{1,0:T(2,128)}, u32[]{:S(2)}) copy-start(f32[2,256]{1,0:T(2,128)} %param.53) | copy-start | bytes 6148
  9.1 94.3 %all-gather.7.cloned.1.call-start = ((), (), s32[]{:S(2)}) async-start(), calls=%async_computation.1 | async-start | bytes 1769472 | tf_op jit(solution)/shard_map/all_gather | solution.py:193
  10.9 92.5 %copy-start.61 = (f32[3,256]{1,0:T(4,128)S(1)}, f32[3,256]{1,0:T(4,128)}, u32[]{:S(2)}) copy-start(f32[3,256]{1,0:T(4,128)} %param.42) | copy-start | bytes 9220
  10.9 160.1 %all-reduce.8.cloned.1.call-start = ((), (), s32[]{:S(2)}) async-start(), calls=%async_computation.2 | async-start | bytes 4194304 | tf_op jit(solution)/shard_map/psum | solution.py:233
  14.6 92.2 %copy-start.44 = (f32[1024]{0:T(1024)}, f32[1024]{0:T(1024)S(1)}, u32[]{:S(2)}) copy-start(f32[1024]{0:T(1024)S(1)} %broadcast_multiply_fusion.1) | copy-start | bytes 12292
  15.3 66.6 %copy-start.49 = (f32[1024]{0:T(1024)}, f32[1024]{0:T(1024)S(1)}, u32[]{:S(2)}) copy-start(f32[1024]{0:T(1024)S(1)} %fusion.10) | copy-start | bytes 12292
  15.4 91.5 %copy-start.53 = (f32[1024]{0:T(1024)}, f32[1024]{0:T(1024)S(1)}, u32[]{:S(2)}) copy-start(f32[1024]{0:T(1024)S(1)} %fusion.123) | copy-start | bytes 12292
  15.4 91.4 %copy-start.47 = (f32[1,1024]{1,0:T(1,128)}, f32[1,1024]{1,0:T(1,128)S(1)}, u32[]{:S(2)}) copy-start(f32[1,1024]{1,0:T(1,128)S(1)} %get-tuple-element.230) | copy-start | bytes 12292
  15.6 91.2 %copy-start.30 = (bf16[10,1024]{1,0:T(8,128)(2,1)}, bf16[10,1024]{1,0:T(8,128)(2,1)S(1)}, u32[]{:S(2)}) copy-start(bf16[10,1024]{1,0:T(8,128)(2,1)S(1)} %convolution_convert_fusion.1) | copy-start | bytes 61444
  85.5 21.6 %copy-start.39 = (bf16[10,1,4,64]{3,2,0,1:T(4,128)(2,1)}, bf16[10,1,4,64]{3,2,0,1:T(4,128)(2,1)S(1)}, u32[]{:S(2)}) copy-start(bf16[10,1,4,64]{3,2,0,1:T(4,128)(2,1)S(1)} %get-tuple-element.227) | copy-start | bytes 15364
  106.9 9.1 %copy-start.14 = (bf16[1024,3,256]{0,2,1:T(8,128)(2,1)}, bf16[1024,3,256]{0,2,1:T(8,128)(2,1)S(1)}, u32[]{:S(2)}) copy-start(bf16[1024,3,256]{0,2,1:T(8,128)(2,1)S(1)} %add_convert_fusion.1) | copy-start | bytes 4718596
  107.2 11.3 %copy-start.11 = (f32[4,512,10]{1,2,0:T(8,128)}, f32[4,512,10]{1,2,0:T(8,128)S(1)}, u32[]{:S(2)}) copy-start(f32[4,512,10]{1,2,0:T(8,128)S(1)} %get-tuple-element.239) | copy-start | bytes 245764
  118.6 15.7 %copy-start.59 = (f32[2,1024]{1,0:T(2,128)S(1)}, f32[2,1024]{1,0:T(2,128)}, u32[]{:S(2)}) copy-start(f32[2,1024]{1,0:T(2,128)} %param.44) | copy-start | bytes 24580
  121.3 100.9 %all-gather.9.cloned.1.call-start = ((), (), s32[]{:S(2)}) async-start(), calls=%async_computation.3 | async-start | bytes 2359296 | tf_op jit(solution)/shard_map/all_gather | solution.py:195
  121.9 149.9 %all-gather.11.cloned.1.call-start = ((), (), s32[]{:S(2)}) async-start(), calls=%async_computation.4 | async-start | bytes 2359296 | tf_op jit(solution)/shard_map/all_gather | solution.py:196
  122.5 210.2 %all-reduce.10.cloned.1.call-start = ((), (), s32[]{:S(2)}) async-start(), calls=%async_computation.5 | async-start | bytes 4194304 | tf_op jit(solution)/shard_map/psum | solution.py:263
  222.2 49.6 %copy-start.62 = (f32[1024]{0:T(1024)S(1)}, f32[1024]{0:T(1024)}, u32[]{:S(2)}) copy-start(f32[1024]{0:T(1024)} %param.46) | copy-start | bytes 12292
  282.6 232.2 %all-reduce.12.cloned.1.call-start = ((), (), s32[]{:S(2)}) async-start(), calls=%async_computation.6 | async-start | bytes 8388608 | tf_op jit(solution)/shard_map/psum | solution.py:242
  352.1 5.8 %copy-start.13 = (f32[4,512,10]{1,2,0:T(8,128)S(1)}, f32[4,512,10]{1,2,0:T(8,128)}, u32[]{:S(2)}) copy-start(f32[4,512,10]{1,2,0:T(8,128)} %copy-done.11) | copy-start | bytes 245764
  352.2 5.8 %copy-start.29 = (f32[4,512]{1,0:T(4,128)S(1)}, f32[4,512]{1,0:T(4,128)}, u32[]{:S(2)}) copy-start(f32[4,512]{1,0:T(4,128)} %get-tuple-element.218) | copy-start | bytes 24580
  352.2 5.8 %copy-start.43 = (f32[4,512]{1,0:T(4,128)S(1)}, f32[4,512]{1,0:T(4,128)}, u32[]{:S(2)}) copy-start(f32[4,512]{1,0:T(4,128)} %copy-done.42) | copy-start | bytes 24580
  352.2 47.8 %copy-start.40 = (bf16[10,1,4,64]{3,2,0,1:T(4,128)(2,1)S(1)}, bf16[10,1,4,64]{3,2,0,1:T(4,128)(2,1)}, u32[]{:S(2)}) copy-start(bf16[10,1,4,64]{3,2,0,1:T(4,128)(2,1)} %copy-done.39) | copy-start | bytes 15364
  352.2 48.8 %copy-start.23 = (f32[10,512]{1,0:T(8,128)S(1)}, f32[10,512]{1,0:T(8,128)}, u32[]{:S(2)}) copy-start(f32[10,512]{1,0:T(8,128)} %copy-done.22) | copy-start | bytes 61444
  357.1 45.8 %copy-start.27 = (f32[4,512]{1,0:T(4,128)S(1)}, f32[4,512]{1,0:T(4,128)}, u32[]{:S(2)}) copy-start(f32[4,512]{1,0:T(4,128)} %get-tuple-element.220) | copy-start | bytes 24580
  399.9 21.6 %copy-start.51 = (f32[2,256]{1,0:T(2,128)}, f32[2,256]{1,0:T(2,128)S(1)}, u32[]{:S(2)}) copy-start(f32[2,256]{1,0:T(2,128)S(1)} %convert_reduce_fusion.2) | copy-start | bytes 6148
  402.9 6.0 %copy-start.16 = (f32[4,64,512]{2,1,0:T(8,128)S(1)}, f32[4,64,512]{2,1,0:T(8,128)}, u32[]{:S(2)}) copy-start(f32[4,64,512]{2,1,0:T(8,128)} %fusion.93) | copy-start | bytes 1572868
  402.9 6.0 %copy-start.38 = (bf16[4,512,10]{1,2,0:T(8,128)(2,1)S(1)}, bf16[4,512,10]{1,2,0:T(8,128)(2,1)}, u32[]{:S(2)}) copy-start(bf16[4,512,10]{1,2,0:T(8,128)(2,1)} %copy-done.37) | copy-start | bytes 122884
  402.9 6.0 %copy-start.41 = (bf16[10,1,4,64]{3,2,0,1:T(4,128)(2,1)S(1)}, bf16[10,1,4,64]{3,2,0,1:T(4,128)(2,1)}, u32[]{:S(2)}) copy-start(bf16[10,1,4,64]{3,2,0,1:T(4,128)(2,1)} %copy-done.39) | copy-start | bytes 15364
  409.9 8.7 %copy-start.19 = (f32[512,4,64]{0,2,1:T(8,128)S(1)}, f32[512,4,64]{0,2,1:T(8,128)}, u32[]{:S(2)}) copy-start(f32[512,4,64]{0,2,1:T(8,128)} %fusion.76) | copy-start | bytes 1572868
  432.3 14.1 %copy-start.24 = (f32[10,512]{1,0:T(8,128)S(1)}, f32[10,512]{1,0:T(8,128)}, u32[]{:S(2)}) copy-start(f32[10,512]{1,0:T(8,128)} %copy-done.22) | copy-start | bytes 61444
  432.3 15.4 %copy-start.10 = (bf16[1024,512]{1,0:T(8,128)(2,1)S(1)}, bf16[1024,512]{1,0:T(8,128)(2,1)}, u32[]{:S(2)}) copy-start(bf16[1024,512]{1,0:T(8,128)(2,1)} %all-gather.5.cloned.1.call-done) | copy-start | bytes 3145732
  432.3 18.8 %copy-start.31 = (bf16[10,1024]{1,0:T(8,128)(2,1)S(1)}, bf16[10,1024]{1,0:T(8,128)(2,1)}, u32[]{:S(2)}) copy-start(bf16[10,1024]{1,0:T(8,128)(2,1)} %copy-done.30) | copy-start | bytes 61444
  432.3 30.0 %copy-start.36 = (f32[10,1024]{1,0:T(8,128)S(1)}, f32[10,1024]{1,0:T(8,128)}, u32[]{:S(2)}) copy-start(f32[10,1024]{1,0:T(8,128)} %param.49) | copy-start | bytes 122884
  432.3 31.6 %copy-start.20 = (f32[128,512]{1,0:T(8,128)S(1)}, f32[128,512]{1,0:T(8,128)}, u32[]{:S(2)}) copy-start(f32[128,512]{1,0:T(8,128)} %param.50) | copy-start | bytes 786436
  447.8 13.3 %copy-start.52 = (f32[512]{0:T(512)S(1)}, f32[512]{0:T(512)}, u32[]{:S(2)}) copy-start(f32[512]{0:T(512)} %get-tuple-element.214) | copy-start | bytes 6148
  448.1 15.8 %copy-start.32 = (f32[128,512]{1,0:T(8,128)S(1)}, f32[128,512]{1,0:T(8,128)}, u32[]{:S(2)}) copy-start(f32[128,512]{1,0:T(8,128)} %param.56) | copy-start | bytes 786436
  448.1 15.8 %copy-start.33 = (f32[128,512]{1,0:T(8,128)S(1)}, f32[128,512]{1,0:T(8,128)}, u32[]{:S(2)}) copy-start(f32[128,512]{1,0:T(8,128)} %param.57) | copy-start | bytes 786436
  453.5 64.1 %copy-start.50 = (f32[1024]{0:T(1024)S(1)}, f32[1024]{0:T(1024)}, u32[]{:S(2)}) copy-start(f32[1024]{0:T(1024)} %copy-done.49) | copy-start | bytes 12292
  453.5 64.1 %copy-start.45 = (f32[1024]{0:T(1024)S(1)}, f32[1024]{0:T(1024)}, u32[]{:S(2)}) copy-start(f32[1024]{0:T(1024)} %copy-done.44) | copy-start | bytes 12292
  453.5 64.1 %copy-start.48 = (f32[1,1024]{1,0:T(1,128)S(1)}, f32[1,1024]{1,0:T(1,128)}, u32[]{:S(2)}) copy-start(f32[1,1024]{1,0:T(1,128)} %copy-done.47) | copy-start | bytes 12292
  453.5 64.1 %copy-start.54 = (f32[1024]{0:T(1024)S(1)}, f32[1024]{0:T(1024)}, u32[]{:S(2)}) copy-start(f32[1024]{0:T(1024)} %copy-done.53) | copy-start | bytes 12292
  (24 other events, 71.8 us)
Sparse Core Ops, SparseCore 0:
  10.8 46.0 all-gather.4
  59.5 43.8 all-gather.6
  121.4 49.5 all-reduce.7
  173.0 49.1 all-gather.8
  224.2 47.6 all-gather.10
  282.7 49.9 all-reduce.9
  432.5 82.2 all-reduce.11
where the time goes:
time: 540 us; the launch traced here: 531 us
  waiting for transfers between devices  236 us (44%)
  blocking collectives  117 us (22%)
  matrix products  78.6 us (15%)
  other arithmetic  49.2 us (9%)
  between operations  20.5 us (4%)
  local copies, waits for them, and re-layouts  17.3 us (3%)
  starting transfers between devices  12.1 us (2%)
    psum x1, waiting for transfers between devices, on_device(): lax.psum(branch_part.astype(jnp.bfloat16), 'tensor').astype(jnp.float32)  49 us
    all_gather x1, waiting for transfers between devices, on_device(): lax.all_gather(up_weight, 'dp', axis=0, tiled=True)  46.3 us
    psum x1, waiting for transfers between devices, on_device(): lax.psum(up_part.astype(jnp.bfloat16), 'tensor').astype(jnp.float32)  43 us
    all_gather x1, waiting for transfers between devices, on_device(): lax.all_gather(down_weight, 'dp', axis=0, tiled=True)  42.4 us
    psum x1, blocking collectives, on_device(): prefix_total = lax.psum(prefix_grad, 'dp')  37.1 us
    psum x1, waiting for transfers between devices, front(): lax.psum(merged_part.astype(jnp.bfloat16), 'tensor').astype(jnp.float32)  36.1 us
    all_gather x1, blocking collectives, on_device(): lax.all_gather(decoder_weight.astype(jnp.bfloat16), 'dp', axis=0, tiled=T...  34.4 us
    all_gather x1, blocking collectives, on_device(): lax.all_gather(merge_weight, 'dp', axis=0, tiled=True)  31.8 us
  transfers between devices with their start and end apart: 7, of which 6 were waited for; matrix products, arithmetic and copies ran while one was open for 8% of the time, Pallas kernels for 0%

commit v1 on v0

--- a/solution.py
+++ b/solution.py
@@ -16,6 +16,28 @@
 ADAM_EPS = 1e-08
 MASKED = -1e30
 GELU_COEF = 0.7978845608028654
+
+
+def in_order(blocks, dim):
+    lengths = list(blocks.shape[1:])
+    lengths[dim] *= blocks.shape[0]
+    return jnp.moveaxis(blocks, 0, dim).reshape(lengths)
+
+
+def ring_gather(x, axis, dim):
+    count = lax.axis_size(axis)
+    pairs = [(i, (i + 1) % count) for i in range(count)]
+    back = [(b, a) for a, b in pairs]
+    lower, upper = ([], [])
+    for step in range(count - 1):
+        if step % 2 == 0:
+            lower.append(lax.ppermute(lower[-1] if lower else x, axis, pairs))
+        else:
+            upper.append(lax.ppermute(upper[-1] if upper else x, axis, back))
+    blocks = jnp.stack([*lower[::-1], x, *upper])
+    shift = lax.axis_index(axis) - len(lower)
+    blocks = blocks[(jnp.arange(count) - shift) % count]
+    return in_order(blocks, dim)
 
 
 def layer_norm(rows, gain, shift):
@@ -195,7 +217,7 @@
         lax.all_gather(up_weight, "dp", axis=0, tiled=True),
         lax.all_gather(down_weight, "dp", axis=0, tiled=True),
         lax.all_gather(encoder_weight.astype(jnp.bfloat16), "dp", axis=0, tiled=True),
-        lax.all_gather(decoder_weight.astype(jnp.bfloat16), "dp", axis=0, tiled=True),
+        ring_gather(decoder_weight.astype(jnp.bfloat16), "dp", 0),
     )
     attend_full, merge_full, up_full, down_full, encoder_full, decoder_full = gathered
     onehot = (prefix_ids[:, None] == jnp.arange(PRE, dtype=jnp.int32)[None, :]).astype(jnp.float32)

time: 540 us -> 544 us (level)
  waiting for transfers between devices: 236 us -> 214 us
  starting transfers between devices: 12.1 us -> 29.9 us
    psum x1, waiting for transfers between devices: 43 us -> 9.66 us  [on_device(): lax.psum(up_part.astype(jnp.bfloat16), 'tensor').astype(jnp.float32)]
    ppermute x0 -> x7, starting transfers between devices: none -> 17.5 us  [the longest x3 16 us: ring_gather(): upper.append(lax.ppermute(upper[-1] if upper else x, axis, back))]
    all_gather x1, starting transfers between devices: 0.04 us -> 12.1 us  [on_device(): lax.all_gather(up_weight, 'dp', axis=0, tiled=True)]
    psum x1, starting transfers between devices: 11.8 us -> 0.04 us  [on_device(): lax.psum(up_part.astype(jnp.bfloat16), 'tensor').astype(jnp.float32)]
    ppermute x0 -> x7, waiting for transfers between devices: none -> 9.15 us  [the longest x4 8.78 us: ring_gather(): lower.append(lax.ppermute(lower[-1] if lower else x, axis, pairs))]
    unnamed x135 -> x130, local copies, waits for them, and re-layouts: 13.4 us -> 12.5 us
  transfers between devices with their start and end apart: 7 -> 14, of which waited for: 6 -> 10; matrix products, arithmetic and copies ran while one was open for 8% -> 9% of each run, Pallas kernels for 0% -> 0%
where the time goes in v1:
time: 544 us; the launch traced here: 534 us
  waiting for transfers between devices  214 us (39%)
  blocking collectives  117 us (22%)
  matrix products  80.8 us (15%)
  other arithmetic  50.6 us (9%)
  starting transfers between devices  29.9 us (5%)
  local copies, waits for them, and re-layouts  21.5 us (4%)
  between operations  20.6 us (4%)
    psum x1, waiting for transfers between devices, on_device(): lax.psum(branch_part.astype(jnp.bfloat16), 'tensor').astype(jnp.float32)  48.2 us
    all_gather x1, waiting for transfers between devices, on_device(): lax.all_gather(up_weight, 'dp', axis=0, tiled=True)  46.3 us
    all_gather x1, waiting for transfers between devices, on_device(): lax.all_gather(down_weight, 'dp', axis=0, tiled=True)  42.4 us
    psum x1, blocking collectives, on_device(): prefix_total = lax.psum(prefix_grad, 'dp')  37.1 us
    psum x1, waiting for transfers between devices, front(): lax.psum(merged_part.astype(jnp.bfloat16), 'tensor').astype(jnp.float32)  35.5 us
    all_gather x1, blocking collectives, on_device(): lax.all_gather(decoder_weight.astype(jnp.bfloat16), 'dp', axis=0, tiled=T...  33.3 us
    all_gather x1, blocking collectives, on_device(): lax.all_gather(merge_weight, 'dp', axis=0, tiled=True)  32.6 us
    all_gather x1, waiting for transfers between devices, on_device(): lax.all_gather(attention_weight, 'dp', axis=0, tiled=True)  22 us
  transfers between devices with their start and end apart: 14, of which 10 were waited for; matrix products, arithmetic and copies ran while one was open for 9% of the time, Pallas kernels for 0%

profile of v1, /device:TPU:0, one launch (start us, length us, event | category | flops | bytes accessed | tf_op | source)
XLA Modules:
  0.0 534.4 jit_solution(17664728354706680140)
XLA Ops:
  7.3 1.8 convert_element_type.156
  10.1 6.1 %collective-permute-start.4 = (bf16[64,2,256]{2,0,1:T(8,128)(2,1)S(1)}, bf16[64,2,256]{2,0,1:T(8,128)(2,1)S(1)}, u32[]{:S(2)}, u32[]{:S(2)}) collective-permute-start(bf16[64,2,256]{2,0,1:T(8,128)(2,1)S(1)} %copy.111), channel_id=1, source_target_pairs={{4,0},{8,4},{12,8},{16,12},{20,16},{24,20},{28,24},{0,28},{5,1},{9... | collective-permute-start | bytes 196616 | tf_op jit(solution)/shard_map/ppermute | solution.py:36
  16.2 1.7 copy.66
  18.0 1.9 convert_reduce_fusion
  22.5 32.6 %all_gather.25 = bf16[1024,256]{1,0:T(8,128)(2,1)S(1)} all-gather(bf16[128,256]{1,0:T(8,128)(2,1)S(1)} %copy-done.39), channel_id=1, replica_groups=mesh['dp'=8,'tensor'=4] {'dp'}, dimensions={0}, use_global_device_ids=true | all-gather | bytes 589824 | tf_op jit(solution)/shard_map/all_gather | solution.py:216
  57.6 5.0 collective-permute-done.1
  62.7 4.8 collective-permute-start.5
  67.5 2.3 collective-permute-done.2
  70.1 5.2 collective-permute-start.6
  82.9 22.0 %all-gather.7.cloned.1.call-done = bf16[1024,3,256]{0,2,1:T(8,128)(2,1)} async-done(((bf16[128,3,256]{0,2,1:T(8,128)(2,1)}), bf16[1024,3,256]{0,2,1:T(8,128)(2,1)}) %all-gather.7.cloned.1.call-update) | async-done | bytes 1572880 | tf_op jit(solution)/shard_map/all_gather | solution.py:215
  104.9 3.5 add_convert_fusion.1
  112.5 1.8 fusion.155
  114.3 1.9 fusion
  117.6 2.5 fusion.21
  120.7 2.1 convolution_convert_fusion
  122.8 12.1 %all-gather.9.cloned.1.call-start = ((), (), s32[]{:S(2)}) async-start(), calls=%async_computation.3 | async-start | bytes 2359296 | tf_op jit(solution)/shard_map/all_gather | solution.py:217
  137.0 35.5 %all-reduce.8.cloned.1.call-done = bf16[1024,1024]{1,0:T(8,128)(2,1)} async-done(((bf16[1024,1024]{1,0:T(8,128)(2,1)}), bf16[1024,1024]{1,0:T(8,128)(2,1)}) %all-reduce.8.cloned.1.call-update) | async-done | bytes 2097168 | tf_op jit(solution)/shard_map/psum | solution.py:255
  172.5 2.3 fusion.148
  174.9 1.9 copy-done.1
  177.4 46.3 %all-gather.9.cloned.1.call-done = bf16[1024,1024]{1,0:T(8,128)(2,1)} async-done(((bf16[128,1024]{1,0:T(8,128)(2,1)}), bf16[1024,1024]{1,0:T(8,128)(2,1)}) %all-gather.9.cloned.1.call-update) | async-done | bytes 2097168 | tf_op jit(solution)/shard_map/all_gather | solution.py:217
  223.7 7.2 %fusion.26 = f32[1024,1024]{1,0:T(8,128)} fusion(bf16[1024,1024]{1,0:T(8,128)(2,1)} %all-gather.9.cloned.1.call-done, f32[1024,1024]{1,0:T(8,128)} %copy-done.1, f32[1024]{0:T(1024)S(1)} %bitcast.218, f32[1024]{0:T(1024)S(1)} %bitcast.209, f32[1024]{0:T(1024)S(1)} %fusion.124, f32[1024]{0:T(1024)S(1)} %broadcast_multiply_fusion), kind=kOutput, calls=%fused_computation.55 | convolution fusion | flops 2152726528 | bytes 10502144 | tf_op jit(solution)/shard_map/dot_general | solution.py:258
  230.9 42.4 %all-gather.11.cloned.1.call-done = bf16[1024,1024]{1,0:T(8,128)(2,1)} async-done(((bf16[128,1024]{1,0:T(8,128)(2,1)}), bf16[1024,1024]{1,0:T(8,128)(2,1)}) %all-gather.11.cloned.1.call-update) | async-done | bytes 2097168 | tf_op jit(solution)/shard_map/all_gather | solution.py:218
  273.3 10.8 %fusion.45 = bf16[1024,1024]{1,0:T(8,128)(2,1)} fusion(bf16[1024,1024]{1,0:T(8,128)(2,1)} %all-gather.9.cloned.1.call-done, f32[1024,1024]{1,0:T(8,128)} %fusion.26, f32[1024]{0:T(1024)S(1)} %copy-done.56, bf16[1024,1024]{1,0:T(8,128)(2,1)} %param.39, bf16[1024,1024]{1,0:T(8,128)(2,1)} %all-gather.11.cloned.1.call-done), kind=kOutput, calls=%fused_computation.74 | convolution fusion | flops 4322230272 | bytes 12587008 | tf_op jit(solution)/shard_map/tf,df->td/dot_general | solution.py:283
  284.2 33.3 %all_gather.28 = bf16[512,2,256]{2,0,1:T(8,128)(2,1)} all-gather(bf16[64,2,256]{2,0,1:T(8,128)(2,1)S(1)} %copy-done.31), channel_id=1, replica_groups=mesh['dp'=8,'tensor'=4] {'dp'}, dimensions={0}, use_global_device_ids=true | all-gather | bytes 589824 | tf_op jit(solution)/shard_map/all_gather | solution.py:276
  317.4 7.1 %fusion.48 = bf16[1024,1024]{1,0:T(8,128)(2,1)} fusion(bf16[1024,1024]{1,0:T(8,128)(2,1)} %all-gather.11.cloned.1.call-done, f32[1024,1024]{1,0:T(8,128)} %fusion.26, f32[1024]{0:T(1024)S(1)} %copy-done.56), kind=kOutput, calls=%fused_computation.75 | convolution fusion | flops 2159017984 | bytes 8392704 | tf_op jit(solution)/shard_map/tf,df->td/dot_general | solution.py:263
  324.5 9.7 %all-reduce.10.cloned.1.call-done = bf16[1024,1024]{1,0:T(8,128)(2,1)} async-done(((bf16[1024,1024]{1,0:T(8,128)(2,1)}), bf16[1024,1024]{1,0:T(8,128)(2,1)}) %all-reduce.10.cloned.1.call-update) | async-done | bytes 2097168 | tf_op jit(solution)/shard_map/psum | solution.py:285
  334.2 3.8 multiply_reduce_fusion.2
  338.9 1.8 fusion.140
  340.7 1.7 add_add_fusion.2
  343.7 2.5 copy-done.4
  352.8 4.9 multiply_reduce_fusion
  362.6 1.8 fusion.112
  366.3 37.1 %psum.56 = bf16[10,2,256]{2,0,1:T(8,128)(2,1)S(1)} all-reduce(f32[10,2,256]{2,0,1:T(8,128)S(1)} %pad_maximum_fusion.2), channel_id=1, replica_groups=mesh['dp'=8,'tensor'=4] {'dp'}, use_global_device_ids=true, to_apply=%region_24.25 | all-reduce | flops 5120 | bytes 30720 | tf_op jit(solution)/shard_map/psum | solution.py:314
  404.1 2.7 multiply_reduce_fusion.5
  406.7 4.8 fusion.64
  414.0 6.8 %multiply_convert_fusion = bf16[4,512,1024]{2,1,0:T(8,128)(2,1)S(1)} fusion(f32[4,512,1024]{2,1,0:T(8,128)} %get-tuple-element.245, f32[4,512,1024]{2,1,0:T(8,128)} %copy-done, f32[4,512]{1,0:T(4,128)S(1)} %add.454, f32[4,512]{1,0:T(4,128)S(1)} %copy-done.22), kind=kLoop, calls=%fused_computation.1 | loop fusion | flops 8388608 | bytes 20987904 | tf_op jit(solution)/shard_map/while/body/eval_jaxpr/convert_element_type | solution.py:142
  422.0 2.1 fusion.67
  425.7 3.8 fusion.84
  431.0 4.9 bitcast_convert_fusion
  435.9 14.0 %all-reduce.2 = (f32[]{:T(128)}, f32[10,512]{1,0:T(8,128)}) all-reduce(f32[]{:T(128)S(6)} %add.464, f32[10,512]{1,0:T(8,128)} %convolution_bitcast_fusion), channel_id=1, replica_groups=mesh['dp'=8,'tensor'=4] {'tensor'}, use_global_device_ids=true, to_apply=%region_28.29 | all-reduce | flops 5121 | bytes 40968 | tf_op jit(solution)/shard_map/psum | solution.py:326
  451.7 1.6 multiply_reduce_fusion.8
  454.6 3.2 multiply_reduce_fusion.4
  466.6 1.6 divide_subtract_fusion.2
  468.2 2.0 divide_subtract_fusion
  470.1 48.2 %all-reduce.12.cloned.1.call-done = (bf16[1024,1024]{1,0:T(8,128)(2,1)}, bf16[1024,1024]{1,0:T(8,128)(2,1)}) async-done(((bf16[1024,1024]{1,0:T(8,128)(2,1)}, bf16[1024,1024]{1,0:T(8,128)(2,1)}), (bf16[1024,1024]{1,0:T(8,128)(2,1)}, bf16[1024,1024]{1,0:T(8,128)(2,1)})) %all-reduce.12.cloned.1.call-update) | async-done | bytes 4194320 | tf_op jit(solution)/shard_map/psum | solution.py:264
  518.4 2.7 fusion.14
  521.1 1.9 fusion.147
  523.2 2.9 fusion.90
  (227 shorter events, 53.3 us)
Async XLA Ops:
  7.2 70.5 %copy-start.17 = (f32[64,2,256]{2,1,0:T(2,128)S(1)}, f32[64,2,256]{2,1,0:T(2,128)}, u32[]{:S(2)}) copy-start(f32[64,2,256]{2,1,0:T(2,128)} %param.52) | copy-start | bytes 393220
  7.2 12.8 %copy-start.5 = (bf16[1024,1024]{1,0:T(8,128)(2,1)S(1)}, bf16[1024,1024]{1,0:T(8,128)(2,1)}, u32[]{:S(2)}) copy-start(bf16[1024,1024]{1,0:T(8,128)(2,1)} %param.38) | copy-start | bytes 6291460
  7.2 13.5 %copy-start.50 = (f32[4,1024]{1,0:T(4,128)S(1)}, f32[4,1024]{1,0:T(4,128)}, u32[]{:S(2)}) copy-start(f32[4,1024]{1,0:T(4,128)} %param.40) | copy-start | bytes 49156
  7.2 15.2 %copy-start.39 = (bf16[128,256]{1,0:T(8,128)(2,1)S(1)}, bf16[128,256]{1,0:T(8,128)(2,1)}, u32[]{:S(2)}) copy-start(bf16[128,256]{1,0:T(8,128)(2,1)} %param.43) | copy-start | bytes 196612
  7.2 47.8 %copy-start.33 = (f32[10,1024]{1,0:T(8,128)S(1)}, f32[10,1024]{1,0:T(8,128)}, u32[]{:S(2)}) copy-start(f32[10,1024]{1,0:T(8,128)} %param.49) | copy-start | bytes 122884
  7.2 47.8 %copy-start.54 = (s32[10]{0:T(128)S(1)}, s32[10]{0:T(128)}, u32[]{:S(2)}) copy-start(s32[10]{0:T(128)} %param.48) | copy-start | bytes 124
  7.3 73.8 %all-gather.5.cloned.1.call-start = ((), (), s32[]{:S(2)}) async-start(), calls=%async_computation | async-start | bytes 1179648 | tf_op jit(solution)/shard_map/all_gather | solution.py:219
  9.1 95.8 %all-gather.7.cloned.1.call-start = ((), (), s32[]{:S(2)}) async-start(), calls=%async_computation.1 | async-start | bytes 1769472 | tf_op jit(solution)/shard_map/all_gather | solution.py:215
  10.1 69.9 %copy-start.30 = (bf16[64,2,256]{2,0,1:T(8,128)(2,1)}, bf16[64,2,256]{2,0,1:T(8,128)(2,1)S(1)}, u32[]{:S(2)}) copy-start(bf16[64,2,256]{2,0,1:T(8,128)(2,1)S(1)} %copy.111) | copy-start | bytes 196612
  10.1 52.6 %collective-permute-start.4 = (bf16[64,2,256]{2,0,1:T(8,128)(2,1)S(1)}, bf16[64,2,256]{2,0,1:T(8,128)(2,1)S(1)}, u32[]{:S(2)}, u32[]{:S(2)}) collective-permute-start(bf16[64,2,256]{2,0,1:T(8,128)(2,1)S(1)} %copy.111), channel_id=1, source_target_pairs={{4,0},{8,4},{12,8},{16,12},{20,16},{24,20},{28,24},{0,28},{5,1},{9... | collective-permute-start | bytes 196616 | tf_op jit(solution)/shard_map/ppermute | solution.py:36
  16.2 39.2 %collective-permute-start = (bf16[64,2,256]{2,0,1:T(8,128)(2,1)S(1)}, bf16[64,2,256]{2,0,1:T(8,128)(2,1)S(1)}, u32[]{:S(2)}, u32[]{:S(2)}) collective-permute-start(bf16[64,2,256]{2,0,1:T(8,128)(2,1)S(1)} %copy.111), channel_id=1, source_target_pairs={{0,4},{4,8},{8,12},{12,16},{16,20},{20,24},{24,28},{28,0},{1,5},{5... | collective-permute-start | bytes 196616 | tf_op jit(solution)/shard_map/ppermute | solution.py:34
  17.9 154.6 %all-reduce.8.cloned.1.call-start = ((), (), s32[]{:S(2)}) async-start(), calls=%async_computation.2 | async-start | bytes 4194304 | tf_op jit(solution)/shard_map/psum | solution.py:255
  18.0 63.0 %copy-start.52 = (f32[512]{0:T(512)S(1)}, f32[512]{0:T(512)}, u32[]{:S(2)}) copy-start(f32[512]{0:T(512)} %param.51) | copy-start | bytes 6148
  19.9 62.6 %copy-start.51 = (f32[2,256]{1,0:T(2,128)S(1)}, f32[2,256]{1,0:T(2,128)}, u32[]{:S(2)}) copy-start(f32[2,256]{1,0:T(2,128)} %param.53) | copy-start | bytes 6148
  20.0 84.9 %copy-start.37 = (f32[1024]{0:T(1024)}, f32[1024]{0:T(1024)S(1)}, u32[]{:S(2)}) copy-start(f32[1024]{0:T(1024)S(1)} %broadcast_multiply_fusion.1) | copy-start | bytes 12292
  20.0 84.9 %copy-start.55 = (f32[3,256]{1,0:T(4,128)S(1)}, f32[3,256]{1,0:T(4,128)}, u32[]{:S(2)}) copy-start(f32[3,256]{1,0:T(4,128)} %param.42) | copy-start | bytes 9220
  20.7 62.0 %copy-start.44 = (f32[1024]{0:T(1024)}, f32[1024]{0:T(1024)S(1)}, u32[]{:S(2)}) copy-start(f32[1024]{0:T(1024)S(1)} %fusion.10) | copy-start | bytes 12292
  21.3 87.0 %copy-start.42 = (f32[1,1024]{1,0:T(1,128)}, f32[1,1024]{1,0:T(1,128)S(1)}, u32[]{:S(2)}) copy-start(f32[1,1024]{1,0:T(1,128)S(1)} %get-tuple-element.230) | copy-start | bytes 12292
  55.3 53.0 %copy-start.25 = (bf16[10,1024]{1,0:T(8,128)(2,1)}, bf16[10,1024]{1,0:T(8,128)(2,1)S(1)}, u32[]{:S(2)}) copy-start(bf16[10,1024]{1,0:T(8,128)(2,1)S(1)} %convolution_convert_fusion.1) | copy-start | bytes 61444
  55.3 53.0 %copy-start.47 = (f32[1024]{0:T(1024)}, f32[1024]{0:T(1024)S(1)}, u32[]{:S(2)}) copy-start(f32[1024]{0:T(1024)S(1)} %fusion.123) | copy-start | bytes 12292
  55.3 19.9 %copy-start.41 = (bf16[64,2,256]{2,0,1:T(8,128)(2,1)}, bf16[64,2,256]{2,0,1:T(8,128)(2,1)S(1)}, u32[]{:S(2)}) copy-start(bf16[64,2,256]{2,0,1:T(8,128)(2,1)S(1)} %collective-permute-done) | copy-start | bytes 196612
  55.4 7.3 %collective-permute-start.1 = (bf16[64,2,256]{2,0,1:T(8,128)(2,1)S(1)}, bf16[64,2,256]{2,0,1:T(8,128)(2,1)S(1)}, u32[]{:S(2)}, u32[]{:S(2)}) collective-permute-start(bf16[64,2,256]{2,0,1:T(8,128)(2,1)S(1)} %collective-permute-done), channel_id=1, source_target_pairs={{0,4},{4,8},{8,12},{12,16},{16,20},{20,24},{24,28},{28,0},{1,5},{5... | collective-permute-start | bytes 196616 | tf_op jit(solution)/shard_map/ppermute | solution.py:34
  62.6 7.1 %collective-permute-start.2 = (bf16[64,2,256]{2,0,1:T(8,128)(2,1)S(1)}, bf16[64,2,256]{2,0,1:T(8,128)(2,1)S(1)}, u32[]{:S(2)}, u32[]{:S(2)}) collective-permute-start(bf16[64,2,256]{2,0,1:T(8,128)(2,1)S(1)} %collective-permute-done.1), channel_id=1, source_target_pairs={{0,4},{4,8},{8,12},{12,16},{16,20},{20,24},{24,28},{28,0},{1,5},{5... | collective-permute-start | bytes 196616 | tf_op jit(solution)/shard_map/ppermute | solution.py:34
  62.7 12.6 %copy-start.40 = (bf16[64,2,256]{2,0,1:T(8,128)(2,1)}, bf16[64,2,256]{2,0,1:T(8,128)(2,1)S(1)}, u32[]{:S(2)}) copy-start(bf16[64,2,256]{2,0,1:T(8,128)(2,1)S(1)} %collective-permute-done.4) | copy-start | bytes 196612
  62.7 7.4 %collective-permute-start.5 = (bf16[64,2,256]{2,0,1:T(8,128)(2,1)S(1)}, bf16[64,2,256]{2,0,1:T(8,128)(2,1)S(1)}, u32[]{:S(2)}, u32[]{:S(2)}) collective-permute-start(bf16[64,2,256]{2,0,1:T(8,128)(2,1)S(1)} %collective-permute-done.4), channel_id=1, source_target_pairs={{4,0},{8,4},{12,8},{16,12},{20,16},{24,20},{28,24},{0,28},{5,1},{9... | collective-permute-start | bytes 196616 | tf_op jit(solution)/shard_map/ppermute | solution.py:36
  69.7 7.1 %collective-permute-start.3 = (bf16[64,2,256]{2,0,1:T(8,128)(2,1)S(1)}, bf16[64,2,256]{2,0,1:T(8,128)(2,1)S(1)}, u32[]{:S(2)}, u32[]{:S(2)}) collective-permute-start(bf16[64,2,256]{2,0,1:T(8,128)(2,1)S(1)} %collective-permute-done.2), channel_id=1, source_target_pairs={{0,4},{4,8},{8,12},{12,16},{16,20},{20,24},{24,28},{28,0},{1,5},{5... | collective-permute-start | bytes 196616 | tf_op jit(solution)/shard_map/ppermute | solution.py:34
  70.1 8.4 %collective-permute-start.6 = (bf16[64,2,256]{2,0,1:T(8,128)(2,1)S(1)}, bf16[64,2,256]{2,0,1:T(8,128)(2,1)S(1)}, u32[]{:S(2)}, u32[]{:S(2)}) collective-permute-start(bf16[64,2,256]{2,0,1:T(8,128)(2,1)S(1)} %collective-permute-done.5), channel_id=1, source_target_pairs={{4,0},{8,4},{12,8},{16,12},{20,16},{24,20},{28,24},{0,28},{5,1},{9... | collective-permute-start | bytes 196616 | tf_op jit(solution)/shard_map/ppermute | solution.py:36
  82.5 25.8 %copy-start.19 = (f32[10,512]{1,0:T(8,128)}, f32[10,512]{1,0:T(8,128)S(1)}, u32[]{:S(2)}) copy-start(f32[10,512]{1,0:T(8,128)S(1)} %fusion.86) | copy-start | bytes 61444
  82.8 25.7 %copy-start.35 = (bf16[10,1,4,64]{3,2,0,1:T(4,128)(2,1)}, bf16[10,1,4,64]{3,2,0,1:T(4,128)(2,1)S(1)}, u32[]{:S(2)}) copy-start(bf16[10,1,4,64]{3,2,0,1:T(4,128)(2,1)S(1)} %get-tuple-element.227) | copy-start | bytes 15364
  108.4 9.1 %copy-start.11 = (bf16[1024,3,256]{0,2,1:T(8,128)(2,1)}, bf16[1024,3,256]{0,2,1:T(8,128)(2,1)S(1)}, u32[]{:S(2)}) copy-start(bf16[1024,3,256]{0,2,1:T(8,128)(2,1)S(1)} %add_convert_fusion.1) | copy-start | bytes 4718596
  122.8 100.9 %all-gather.9.cloned.1.call-start = ((), (), s32[]{:S(2)}) async-start(), calls=%async_computation.3 | async-start | bytes 2359296 | tf_op jit(solution)/shard_map/all_gather | solution.py:217
  135.0 138.4 %all-gather.11.cloned.1.call-start = ((), (), s32[]{:S(2)}) async-start(), calls=%async_computation.4 | async-start | bytes 2359296 | tf_op jit(solution)/shard_map/all_gather | solution.py:218
  135.5 198.6 %all-reduce.10.cloned.1.call-start = ((), (), s32[]{:S(2)}) async-start(), calls=%async_computation.5 | async-start | bytes 4194304 | tf_op jit(solution)/shard_map/psum | solution.py:285
  174.9 48.8 %copy-start.53 = (f32[1,1024]{1,0:T(1,128)S(1)}, f32[1,1024]{1,0:T(1,128)}, u32[]{:S(2)}) copy-start(f32[1,1024]{1,0:T(1,128)} %get-tuple-element.231) | copy-start | bytes 12292
  223.7 49.6 %copy-start.56 = (f32[1024]{0:T(1024)S(1)}, f32[1024]{0:T(1024)}, u32[]{:S(2)}) copy-start(f32[1024]{0:T(1024)} %param.46) | copy-start | bytes 12292
  230.9 53.3 %copy-start.31 = (bf16[64,2,256]{2,0,1:T(8,128)(2,1)S(1)}, bf16[64,2,256]{2,0,1:T(8,128)(2,1)}, u32[]{:S(2)}) copy-start(bf16[64,2,256]{2,0,1:T(8,128)(2,1)} %copy-done.30) | copy-start | bytes 196612
  284.1 234.2 %all-reduce.12.cloned.1.call-start = ((), (), s32[]{:S(2)}) async-start(), calls=%async_computation.6 | async-start | bytes 8388608 | tf_op jit(solution)/shard_map/psum | solution.py:264
  352.8 7.1 %copy-start.24 = (f32[4,512]{1,0:T(4,128)S(1)}, f32[4,512]{1,0:T(4,128)}, u32[]{:S(2)}) copy-start(f32[4,512]{1,0:T(4,128)} %get-tuple-element.218) | copy-start | bytes 24580
  352.8 9.7 %copy-start.22 = (f32[4,512]{1,0:T(4,128)S(1)}, f32[4,512]{1,0:T(4,128)}, u32[]{:S(2)}) copy-start(f32[4,512]{1,0:T(4,128)} %get-tuple-element.220) | copy-start | bytes 24580
  414.0 8.0 %copy-start.16 = (f32[512,4,64]{0,2,1:T(8,128)S(1)}, f32[512,4,64]{0,2,1:T(8,128)}, u32[]{:S(2)}) copy-start(f32[512,4,64]{0,2,1:T(8,128)} %fusion.76) | copy-start | bytes 1572868
  435.9 15.4 %copy-start.10 = (bf16[1024,512]{1,0:T(8,128)(2,1)S(1)}, bf16[1024,512]{1,0:T(8,128)(2,1)}, u32[]{:S(2)}) copy-start(bf16[1024,512]{1,0:T(8,128)(2,1)} %all-gather.5.cloned.1.call-done) | copy-start | bytes 3145732
  435.9 32.3 %copy-start.18 = (f32[128,512]{1,0:T(8,128)S(1)}, f32[128,512]{1,0:T(8,128)}, u32[]{:S(2)}) copy-start(f32[128,512]{1,0:T(8,128)} %param.50) | copy-start | bytes 786436
  451.7 16.5 %copy-start.28 = (f32[128,512]{1,0:T(8,128)S(1)}, f32[128,512]{1,0:T(8,128)}, u32[]{:S(2)}) copy-start(f32[128,512]{1,0:T(8,128)} %param.56) | copy-start | bytes 786436
  451.7 16.5 %copy-start.29 = (f32[128,512]{1,0:T(8,128)S(1)}, f32[128,512]{1,0:T(8,128)}, u32[]{:S(2)}) copy-start(f32[128,512]{1,0:T(8,128)} %param.57) | copy-start | bytes 786436
  457.8 63.3 %copy-start.45 = (f32[1024]{0:T(1024)S(1)}, f32[1024]{0:T(1024)}, u32[]{:S(2)}) copy-start(f32[1024]{0:T(1024)} %copy-done.44) | copy-start | bytes 12292
  457.8 63.3 %copy-start.38 = (f32[1024]{0:T(1024)S(1)}, f32[1024]{0:T(1024)}, u32[]{:S(2)}) copy-start(f32[1024]{0:T(1024)} %copy-done.37) | copy-start | bytes 12292
  457.8 63.3 %copy-start.43 = (f32[1,1024]{1,0:T(1,128)S(1)}, f32[1,1024]{1,0:T(1,128)}, u32[]{:S(2)}) copy-start(f32[1,1024]{1,0:T(1,128)} %copy-done.42) | copy-start | bytes 12292
  457.8 63.3 %copy-start.48 = (f32[1024]{0:T(1024)S(1)}, f32[1024]{0:T(1024)}, u32[]{:S(2)}) copy-start(f32[1024]{0:T(1024)} %copy-done.47) | copy-start | bytes 12292
  (25 other events, 84.8 us)
Sparse Core Ops, SparseCore 0:
  10.8 45.4 all-gather.4
  58.9 45.9 all-gather.6
  122.9 49.5 all-reduce.7
  174.5 49.1 all-gather.8
  225.7 47.6 all-gather.10
  284.2 49.9 all-reduce.9
  436.0 82.2 all-reduce.11
